TPU v7x, 8 devices: a whole 2x2x1 slice. The times are simulated.
8 devices in a mesh: dp: 1 (over z), sp: 2 (over y), tp: 4 (over x, core).
Axes of the slice: x: 2, y: 2, z: 1, core: 2. Of those that a mesh axis runs over, the one named last changes fastest.
Arguments:
- hidden: bfloat16 [256, 2048], P('dp')
- new_pos: int32 [256], P('dp')
- k_self: bfloat16 [256, 256, 8, 128], P('dp', 'sp', 'tp')
- v_self: bfloat16 [256, 256, 8, 128], P('dp', 'sp', 'tp')
- k_cross: bfloat16 [256, 512, 8, 128], P('dp', None, 'tp')
- v_cross: bfloat16 [256, 512, 8, 128], P('dp', None, 'tp')
- xvalid: int32 [256, 512], P('dp')
- rowmask: int32 [256], P('dp')
- self_attn_norm: bfloat16 [2048], replicated
- self_wq: bfloat16 [2048, 2048], P(None, 'tp')
- self_wk: bfloat16 [2048, 1024], P(None, 'tp')
- self_wv: bfloat16 [2048, 1024], P(None, 'tp')
- self_wo: bfloat16 [2048, 2048], P('tp')
- self_mlp_norm: bfloat16 [2048], replicated
- self_wgate: bfloat16 [2048, 6144], P(None, 'tp')
- self_wup: bfloat16 [2048, 6144], P(None, 'tp')
- self_wdown: bfloat16 [6144, 2048], P('tp')
- cross_attn_norm: bfloat16 [2048], replicated
- cross_wq: bfloat16 [2048, 2048], P(None, 'tp')
- cross_qnorm: bfloat16 [128], replicated
- cross_wo: bfloat16 [2048, 2048], P('tp')
- cross_gates: float32 [2], replicated
- cross_mlp_norm: bfloat16 [2048], replicated
- cross_wgate: bfloat16 [2048, 6144], P(None, 'tp')
- cross_wup: bfloat16 [2048, 6144], P(None, 'tp')
- cross_wdown: bfloat16 [6144, 2048], P('tp')
Outputs:
- output 1: bfloat16 [256, 2048], P('dp')
- output 2: bfloat16 [256, 256, 8, 128], P('dp', 'sp', 'tp')
- output 3: bfloat16 [256, 256, 8, 128], P('dp', 'sp', 'tp')
All inputs are finite; a program needn't handle non-finite values.
Results may differ from a plain program's by a relative error of at most 0.0146321.
Values sent between devices are 32-bit elements.
A program may use at most 1 GiB of HBM per device.

v0:
```python
import functools
import math
import numpy as np
import jax
import jax.numpy as jnp
from jax import lax
from jax.experimental import pallas as pl
from jax.experimental.pallas import tpu as pltpu
from jax.sharding import PartitionSpec as P

NORM_EPS = 1e-5
ROPE_THETA = 500000.0
ROPE_FACTOR = 8.0
LOW_FREQ = 1.0
HIGH_FREQ = 4.0
ORIG_CTX = 8192.0
NEG_BIG = -1e30

BF = jnp.bfloat16
F32 = jnp.float32
D = 128
HL = 4
KL = 2
NB = 256
NH = 128
NQ = 64
HID = 2048
HQ = NQ // 2
NCH = 4
W = HID // NCH
VMEM_MAX = 66 * 1024 * 1024 - 2 * 1024 * 1024
MESH = pl.DeviceIdType.MESH
ANY = pl.BlockSpec(memory_space=pl.ANY)
VM = pl.BlockSpec(memory_space=pltpu.VMEM)


def rope_freqs(head_dim):
    inv_freq = 1.0 / (ROPE_THETA ** (np.arange(0, head_dim, 2) / head_dim))
    wavelen = 2.0 * math.pi / inv_freq
    smooth = (ORIG_CTX / wavelen - LOW_FREQ) / (HIGH_FREQ - LOW_FREQ)
    mid_freq = (1.0 - smooth) * inv_freq / ROPE_FACTOR + smooth * inv_freq
    scaled = np.where(wavelen > ORIG_CTX / LOW_FREQ, inv_freq / ROPE_FACTOR, mid_freq)
    scaled = np.where(wavelen < ORIG_CTX / HIGH_FREQ, inv_freq, scaled)
    return np.concatenate([scaled, scaled]).astype(np.float32)[None, :]


def norm32(vals32, gain32):
    inv = lax.rsqrt(jnp.mean(vals32 * vals32, axis=-1, keepdims=True) + NORM_EPS)
    return (vals32 * inv * gain32).astype(BF)


def dot(a, b):
    return jnp.dot(a, b, preferred_element_type=F32)


def dot_nt(a, b):
    return lax.dot_general(a, b, (((1,), (1,)), ((), ())), preferred_element_type=F32)


def attend(lhs, keys, vals, valid):
    first = lax.broadcasted_iota(jnp.int32, (8, D), 0) < HL
    s = [dot_nt(a, k) * (D ** -0.5) for a, k in zip(lhs, keys)]
    s = [jnp.where(ok, x, NEG_BIG) for ok, x in zip(valid, s)]
    m = [jnp.max(x, axis=-1, keepdims=True) for x in s]
    p = [jnp.where(ok, jnp.exp(x - t), 0.0) for ok, x, t in zip(valid, s, m)]
    l = [jnp.sum(x, axis=-1, keepdims=True) for x in p]
    o = [dot(x.astype(BF), v) for x, v in zip(p, vals)]
    return m, l, [jnp.where(first, x[:, :D], x[:, D:]) for x in o]


def pair_lhs(q_ref, b0):
    q16 = q_ref[pl.ds(pl.multiple_of(b0 * 8, 16), 16), :]
    return jnp.concatenate([q16[:8], q16[8:]], axis=1).astype(BF)


def column(vec, first, rows):
    n = vec.shape[1]
    at = lax.broadcasted_iota(jnp.int32, (rows, n), 1) == lax.broadcasted_iota(jnp.int32, (rows, n), 0) + first
    return jnp.sum(jnp.where(at, vec, 0.0), axis=1, keepdims=True)


def spread_heads(ref, heads, start, rows):
    odd = (lax.broadcasted_iota(jnp.int32, (rows, D), 0) % 2) == 1
    for h in range(HL):
        ref[pl.ds(start * 8 + h, rows, stride=8), :] = jnp.where(odd, 0.0, heads[h])
        ref[pl.ds(start * 8 + HL + h, rows, stride=8), :] = jnp.where(odd, heads[h], 0.0)


SR = 16


def self_kernel(pos_ref, posv_ref, freq_ref, g_ref, hid_hbm, wq_hbm, wk_hbm, wv_hbm, k_hbm, v_hbm,
                ko_hbm, vo_hbm, o_hbm, st_hbm,
                hid, wq, wk, wv, wsem, kbuf, vbuf, isem, osem, qs, kn, vn, o_ref, st_ref, rsem):
    T2 = k_hbm.shape[1]
    steps = NB // SR
    first_pos = lax.axis_index("sp") * (T2 // KL)
    loads = [pltpu.make_async_copy(a, b, wsem.at[n])
             for n, (a, b) in enumerate(((hid_hbm, hid), (wq_hbm, wq), (wk_hbm, wk), (wv_hbm, wv)))]
    for cp in loads:
        cp.start()

    def into(i):
        rows = pl.ds(pl.multiple_of(i * SR, SR), SR)
        return (pltpu.make_async_copy(k_hbm.at[rows], kbuf.at[i], isem.at[0, i]),
                pltpu.make_async_copy(v_hbm.at[rows], vbuf.at[i], isem.at[1, i]))

    def out_of(i):
        rows = pl.ds(pl.multiple_of(i * SR, SR), SR)
        return (pltpu.make_async_copy(kbuf.at[i], ko_hbm.at[rows], osem.at[0, i]),
                pltpu.make_async_copy(vbuf.at[i], vo_hbm.at[rows], osem.at[1, i]))

    early = 5
    for i in range(early):
        for cp in into(i):
            cp.start()

    with jax.named_scope("qkv"):
        angle = column(posv_ref[...].astype(F32).reshape(1, NB), 0, NB) * freq_ref[...]
        cos, sin = jnp.cos(angle), jnp.sin(angle)
        sin = jnp.where(lax.broadcasted_iota(jnp.int32, (NB, D), 1) < D // 2, -sin, sin)

        def rope(part):
            part = part.astype(BF).astype(F32)
            return (part * cos + pltpu.roll(part, D // 2, 1) * sin).astype(BF).astype(F32)

        loads[0].wait()
        loads[1].wait()
        for i in range(early, steps):
            for cp in into(i):
                cp.start()
        x = norm32(hid[...].astype(F32), g_ref[...].astype(F32).reshape(1, HID))
        q = dot(x, wq[...])
        spread_heads(qs, [rope(q[:, h * D:(h + 1) * D]) for h in range(HL)], 0, NB)
        loads[2].wait()
        k = dot(x, wk[...])
        loads[3].wait()
        v = dot(x, wv[...])
        for h in range(KL):
            kn[pl.ds(h, NB, stride=KL), :] = rope(k[:, h * D:(h + 1) * D])
            vn[pl.ds(h, NB, stride=KL), :] = v[:, h * D:(h + 1) * D].astype(BF).astype(F32)
    st_ref[...] = jnp.zeros_like(st_ref)

    col = lax.broadcasted_iota(jnp.int32, (8, T2), 1)
    row = lax.broadcasted_iota(jnp.int32, (8, T2), 0)
    tok = col // KL
    head_ok = (col % KL) == ((row % HL) // (HL // KL))
    lane = lax.broadcasted_iota(jnp.int32, (8, D), 1)
    i16 = lax.broadcasted_iota(jnp.int32, (16, D), 0)

    def patch(new_ref, dst_ref, slot, r, b, lp):
        base = pl.multiple_of((jnp.clip(lp, 0, T2 // KL - 1) // 8) * 16, 16)
        fresh = jnp.where(i16 % 2 == 0, new_ref[pl.ds(2 * b, 1), :], new_ref[pl.ds(2 * b + 1, 1), :])
        old = dst_ref[slot, r, pl.ds(base, 16), :].astype(F32)
        dst_ref[slot, r, pl.ds(base, 16), :] = jnp.where(base + i16 - i16 % 2 == 2 * lp, fresh, old).astype(BF)

    def body(i, _):
        for cp in into(i):
            cp.wait()
        lps = [pos_ref[i * SR + r] - first_pos for r in range(SR)]
        for r in range(SR):
            patch(kn, kbuf, i, r, i * SR + r, lps[r])
            patch(vn, vbuf, i, r, i * SR + r, lps[r])
        pairs = range(SR // 2)
        both = lambda buf, p: jnp.concatenate([buf[i, 2 * p], buf[i, 2 * p + 1]], axis=1)
        m, l, o = attend([pair_lhs(qs, i * SR + 2 * p) for p in pairs], [both(kbuf, p) for p in pairs],
                         [both(vbuf, p) for p in pairs],
                         [head_ok & (tok <= jnp.where(row < HL, lps[2 * p], lps[2 * p + 1])) for p in pairs])
        half = i // (NH // SR)
        srow = pl.ds(pl.multiple_of(half * 8, 8), 8)
        st = st_ref[srow, :]
        for p in pairs:
            o_ref[pl.ds(pl.multiple_of(i * SR * HL + 8 * p, 8), 8), :] = o[p]
            at = (i - half * (NH // SR)) * (SR // 2) + p
            st = jnp.where(lane == at, m[p], jnp.where(lane == at + NQ, l[p], st))
        st_ref[srow, :] = st
        for cp in out_of(i):
            cp.start()
        return 0

    results = []
    for i in range(4):
        with jax.named_scope("steps"):
            lax.fori_loop(i * (steps // 4), (i + 1) * (steps // 4), body, 0)
        part = pl.ds(i * (NB * HL // 4), NB * HL // 4)
        results.append(pltpu.make_async_copy(o_ref.at[part], o_hbm.at[part], rsem.at[i]))
        results[-1].start()
    results.append(pltpu.make_async_copy(st_ref, st_hbm, rsem.at[4]))
    results[-1].start()
    with jax.named_scope("drain"):
        for i in range(steps):
            for cp in out_of(i):
                cp.wait()
        for cp in results:
            cp.wait()


def self_attention(new_pos, g1, hidden, wq, wk, wv, k_self, v_self):
    T2 = k_self.shape[1]
    return pl.pallas_call(
        self_kernel,
        in_specs=[pl.BlockSpec(memory_space=pltpu.SMEM), VM, VM, VM] + [ANY] * 6,
        out_specs=[ANY] * 4,
        scratch_shapes=[pltpu.VMEM(hidden.shape, BF), pltpu.VMEM(wq.shape, BF), pltpu.VMEM(wk.shape, BF),
                        pltpu.VMEM(wv.shape, BF), pltpu.SemaphoreType.DMA((4,)),
                        pltpu.VMEM((NB // SR, SR, T2, D), BF), pltpu.VMEM((NB // SR, SR, T2, D), BF),
                        pltpu.SemaphoreType.DMA((2, NB // SR)), pltpu.SemaphoreType.DMA((2, NB // SR)),
                        pltpu.VMEM((NB * 8, D), F32), pltpu.VMEM((NB * KL, D), F32), pltpu.VMEM((NB * KL, D), F32),
                        pltpu.VMEM((NB * HL, D), F32), pltpu.VMEM((16, D), F32), pltpu.SemaphoreType.DMA((5,))],
        out_shape=[jax.ShapeDtypeStruct(k_self.shape, BF), jax.ShapeDtypeStruct(v_self.shape, BF),
                   jax.ShapeDtypeStruct((NB * HL, D), F32), jax.ShapeDtypeStruct((16, D), F32)],
        compiler_params=pltpu.CompilerParams(vmem_limit_bytes=VMEM_MAX),
        name="self_attn",
    )(new_pos, new_pos, jnp.asarray(rope_freqs(D)), g1, hidden, wq, wk, wv, k_self, v_self)


def peers():
    sp, tp = lax.axis_index("sp"), lax.axis_index("tp")
    core = lax.rem(tp, 2)
    return dict(sp=sp, core=core, y={"sp": 1 - sp}, c={"tp": tp + 1 - 2 * core}, x={"tp": lax.rem(tp + 2, 4)})


def entry_barrier(pe):
    barrier = pltpu.get_barrier_semaphore()
    for name in ("y", "c", "x"):
        pl.semaphore_signal(barrier, inc=1, device_id=pe[name], device_id_type=MESH)
    pl.semaphore_wait(barrier, 3)


def rcopy(src, dst, ssem, rsem, dev):
    return pltpu.make_async_remote_copy(src_ref=src, dst_ref=dst, send_sem=ssem, recv_sem=rsem,
                                        device_id=dev, device_id_type=MESH)


class TpSum:
    def __init__(self, pe, half, bufs):
        snd, rcv, chip, xr, sems = bufs
        self.snd, self.rcv, self.chip, self.xr = (b.at[half] for b in (snd, rcv, chip, xr))
        at = lambda n, j: sems.at[half, n, j]
        self.to_core = [rcopy(self.snd.at[j], self.rcv.at[j], at(0, j), at(1, j), pe["c"]) for j in range(NCH)]
        self.to_chip = [rcopy(self.chip.at[j], self.xr.at[j], at(2, j), at(3, j), pe["x"]) for j in range(NCH)]

    def start(self, compute):
        for j in range(NCH):
            part = compute(j)
            self.snd[j] = part[HQ:]
            self.chip[j] = part[:HQ]
            self.to_core[j].start()

    def forward(self):
        for j in range(NCH):
            self.to_core[j].wait_recv()
            self.chip[j] = self.chip[j] + self.rcv[j]
            self.to_chip[j].start()

    def close(self, finish):
        for j in range(NCH):
            self.to_chip[j].wait_recv()
            finish(j, self.chip[j] + self.xr[j])
        for j in range(NCH):
            self.to_core[j].wait_send()
            self.to_chip[j].wait_send()


class Share:
    def __init__(self, pe, half, x_ref, snd, rcv, sems):
        rows = pl.ds(half * HQ, HQ)
        self.snd, self.rcv, self.x = snd.at[rows], rcv.at[rows], x_ref.at[half]
        self.copy = rcopy(self.snd, self.rcv, sems.at[0, half], sems.at[1, half], pe["c"])

    def start(self, own):
        self.snd[...] = own.astype(F32)
        self.copy.start()
        self.x[pl.ds(0, HQ), :] = own

    def finish(self):
        self.copy.wait()
        self.x[pl.ds(HQ, HQ), :] = self.rcv[...].astype(BF)


def mlp_act(x_ref, wg, wu, act, chunks):
    step = act.shape[1] // 3
    for c in chunks:
        s = slice(c * step, (c + 1) * step)
        gate = dot(x_ref[...], wg[:, s]).astype(BF).astype(F32)
        up = dot(x_ref[...], wu[:, s]).astype(BF).astype(F32)
        act[:, s] = (gate * jax.nn.sigmoid(gate) * up).astype(BF)


def cols(j):
    return slice(j * W, (j + 1) * W)


def heads_to_lanes(ref, starts, rows):
    parts = [jnp.concatenate([ref[pl.ds(s * HL + h, rows, stride=HL), :] for h in range(HL)], axis=1) for s in starts]
    return jnp.concatenate(parts, axis=0).astype(BF)


CR = 8
NR = 5
RC = NQ // NCH
XB = 2 * RC // CR


def rest_kernel(o_hbm, st_ref, hid_hbm, g2_ref, g3_ref, qn_ref, g4_ref, gates_ref, mask_ref, valid_hbm,
                wo_hbm, wg_hbm, wu_hbm, wd_hbm, wq_hbm, wo2_hbm, wg2_hbm, wu2_hbm, wd2_hbm, k_hbm, v_hbm,
                out_hbm,
                out_ref, rsem, wo, wg, wu, wd, wq, wo2, wsem, kbuf, vbuf, ksem, osnd, orcv, sts, str_, ysem, hown, att, valid, cnt,
                qx, xbuf, act, hres, h2, fin, yr, cr, gsem,
                a0, a1, a2, a3, asem, b0, b1, b2, b3, bsem, c0, c1, c2, c3, csem, dsem,
                s0, s1, ssem, t0, t1, tsem, esem):
    pe = peers()
    sp, core = pe["sp"], pe["core"]
    T2 = k_hbm.shape[1]
    half = NH * HL
    blocks = NH // CR

    local = [pltpu.make_async_copy(o_hbm.at[pl.ds(pl.multiple_of((1 - sp) * half, half), half)], osnd, wsem.at[6]),
             pltpu.make_async_copy(o_hbm.at[pl.ds(pl.multiple_of(sp * half, half), half)], att, wsem.at[7]),
             pltpu.make_async_copy(hid_hbm.at[pl.ds(pl.multiple_of(sp * NH + core * NQ, NQ), NQ)], hown, wsem.at[8]),
             pltpu.make_async_copy(valid_hbm.at[pl.ds(pl.multiple_of(sp * NH, NH), NH)], valid, wsem.at[9])]
    pairs = ((wo_hbm, wo), (wg_hbm, wg), (wu_hbm, wu), (wd_hbm, wd), (wq_hbm, wq), (wo2_hbm, wo2))
    loads = [pltpu.make_async_copy(a, b, wsem.at[n]) for n, (a, b) in enumerate(pairs)]
    for cp in local:
        cp.start()

    def block_row(t):
        chunk, of_core, sub = t // XB, (t % XB) // (XB // 2), t % (XB // 2)
        return of_core * NQ + chunk * RC + sub * CR

    def kv_loads(t):
        rows, slot = pl.ds(pl.multiple_of(sp * NH + block_row(t), CR), CR), t % NR
        return (pltpu.make_async_copy(k_hbm.at[rows], kbuf.at[slot], ksem.at[0, slot]),
                pltpu.make_async_copy(v_hbm.at[rows], vbuf.at[slot], ksem.at[1, slot]))

    with jax.named_scope("enter"):
        entry_barrier(pe)
    both = st_ref[...]
    mine = jnp.where(sp == 0, both[:8], both[8:])
    sts[...] = jnp.where(sp == 0, both[8:], both[:8])
    local[0].wait()
    cp_s = rcopy(sts, str_, ysem.at[0, 4], ysem.at[1, 4], pe["y"])
    cp_s.start()

    def quarter(h, c):
        rows = pl.ds((c * NQ + h * HQ) * HL, HQ * HL)
        return rcopy(osnd.at[rows], orcv.at[rows], ysem.at[0, 2 * h + c], ysem.at[1, 2 * h + c], pe["y"])

    quarters = [quarter(h, c) for h in range(2) for c in range(2)]
    for cp in quarters:
        cp.start()
    for cp in local[1:]:
        cp.wait()
    for cp in loads:
        cp.start()
    for t in range(NR):
        for cp in kv_loads(t):
            cp.start()
    some = jnp.sum((valid[...] > 0).astype(jnp.int32), axis=1, keepdims=True)
    cnt[...] = jnp.broadcast_to(some, cnt.shape)
    row_scale = column(mask_ref[...].astype(F32).reshape(1, NB), sp * NH + core * NQ, NQ)
    gate0 = jnp.tanh(jnp.full((8, D), gates_ref[0], F32))[0:1, 0:1] * row_scale
    gate1 = jnp.tanh(jnp.full((8, D), gates_ref[1], F32))[0:1, 0:1] * row_scale
    gain = lambda ref: ref[...].astype(F32).reshape(1, HID)
    owned = [slice(h * HQ, (h + 1) * HQ) for h in range(2)]
    sum1 = [TpSum(pe, h, (a0, a1, a2, a3, asem)) for h in range(2)]
    sum2 = [TpSum(pe, h, (b0, b1, b2, b3, bsem)) for h in range(2)]
    sum4 = [TpSum(pe, h, (a0, a1, a2, a3, esem)) for h in range(2)]
    share1 = [Share(pe, h, xbuf, s0, s1, ssem) for h in range(2)]
    share2 = [Share(pe, h, xbuf, t0, t1, tsem) for h in range(2)]

    cp_s.wait()
    theirs = str_[...]
    top = jnp.maximum(mine, theirs)
    f1, f2 = jnp.exp(mine - top), jnp.exp(theirs - top)
    den = pltpu.roll(mine, NQ, 1) * f1 + pltpu.roll(theirs, NQ, 1) * f2
    w1, w2 = f1 / den, f2 / den

    def combine(h):
        for c in range(2):
            quarters[2 * h + c].wait()
            for p in range((c * NQ + h * HQ) // 2, (c * NQ + h * HQ + HQ) // 2):
                s = pl.ds(8 * p, 8)
                att[s, :] = att[s, :] * w1[:, p:p + 1] + orcv[s, :] * w2[:, p:p + 1]
        return heads_to_lanes(att, (core * NQ + h * HQ, (1 - core) * NQ + h * HQ), HQ)

    def close1(h):
        def done(j, total):
            hres[owned[h], cols(j)] = (hown[owned[h], cols(j)].astype(F32) + total).astype(BF)

        sum1[h].close(done)
        share1[h].start(norm32(hres[owned[h], :].astype(F32), gain(g2_ref)))

    def mlp_down(h, total):
        total.start(lambda j: dot(act[h], wd[:, cols(j)]))

    def mlp(h, total):
        mlp_act(xbuf.at[h], wg, wu, act.at[h], range(3))
        mlp_down(h, total)

    def close2(h):
        def done(j, total):
            h2[owned[h], cols(j)] = (hres[owned[h], cols(j)].astype(F32) + total).astype(BF)

        sum2[h].close(done)
        share2[h].start(norm32(h2[owned[h], :].astype(F32), gain(g3_ref)))

    def cross_q(h):
        share2[h].finish()
        q = dot(xbuf[h], wq[...])
        qgain = qn_ref[...].astype(F32).reshape(1, D)
        heads = [norm32(q[:, n * D:(n + 1) * D].astype(BF).astype(F32), qgain).astype(F32) for n in range(HL)]
        spread_heads(qx, [x[:HQ] for x in heads], core * NQ + h * HQ, HQ)
        spread_heads(qx, [x[HQ:] for x in heads], (1 - core) * NQ + h * HQ, HQ)

    with jax.named_scope("out_a"):
        lhs0 = combine(0)
        loads[0].wait()
        sum1[0].start(lambda j: dot(lhs0, wo[:, cols(j)]))
    with jax.named_scope("out_b"):
        sum1[0].forward()
        lhs1 = combine(1)
        sum1[1].start(lambda j: dot(lhs1, wo[:, cols(j)]))
        sum1[1].forward()
    with jax.named_scope("close1_a"):
        close1(0)
    with jax.named_scope("share1_a"):
        share1[0].finish()
    for cp in loads[1:4]:
        cp.wait()
    with jax.named_scope("mlp_a"):
        mlp(0, sum2[0])
        sum2[0].forward()
    with jax.named_scope("close1_b"):
        close1(1)
    with jax.named_scope("share1_b"):
        share1[1].finish()
    with jax.named_scope("mlp_b"):
        mlp(1, sum2[1])
        sum2[1].forward()
    loads2 = [pltpu.make_async_copy(a, b, wsem.at[1 + n])
              for n, (a, b) in enumerate(((wg2_hbm, wg), (wu2_hbm, wu), (wd2_hbm, wd)))]
    for cp in loads2:
        cp.start()
    with jax.named_scope("close2_a"):
        close2(0)
    loads[4].wait()
    with jax.named_scope("q_a"):
        cross_q(0)
    loads[5].wait()

    col = lax.broadcasted_iota(jnp.int32, (8, T2), 1)
    row = lax.broadcasted_iota(jnp.int32, (8, T2), 0)
    tok = col // KL
    head_ok = (col % KL) == ((row % HL) // (HL // KL))
    first = lax.broadcasted_iota(jnp.int32, (8, D), 0) < HL

    def block(t, _):
        slot = t % NR
        r0 = pl.multiple_of(block_row(t), CR)
        for cp in kv_loads(t):
            cp.wait()
        ps = range(CR // 2)
        lane_pair = lambda buf, p: jnp.concatenate([buf[slot, 2 * p], buf[slot, 2 * p + 1]], axis=1)
        n8 = cnt[pl.ds(r0, CR), :]
        limit = [jnp.concatenate([jnp.where(first, n8[2 * p:2 * p + 1], n8[2 * p + 1:2 * p + 2])] * (T2 // D), axis=1)
                 for p in ps]
        m, l, o = attend([pair_lhs(qx, r0 + 2 * p) for p in ps], [lane_pair(kbuf, p) for p in ps],
                         [lane_pair(vbuf, p) for p in ps], [head_ok & (tok < n) for n in limit])
        for p in ps:
            att[pl.ds(pl.multiple_of(r0 * HL + 8 * p, 8), 8), :] = o[p] / l[p]

        @pl.when(t + NR < blocks)
        def _():
            for cp in kv_loads(t + NR):
                cp.start()
        return 0

    to_core = [rcopy(c0.at[j], c1.at[j], csem.at[0, j], csem.at[1, j], pe["c"]) for j in range(NCH)]
    to_chip = [rcopy(c2.at[j], c3.at[j], csem.at[2, j], csem.at[3, j], pe["x"]) for j in range(NCH)]
    share = [rcopy(s0.at[pl.ds(j * RC, RC)], s1.at[pl.ds(j * RC, RC)], dsem.at[0, j], dsem.at[1, j], pe["c"])
             for j in range(NCH)]

    def pass_chip(j):
        to_core[j].wait_recv()
        c2[j] = c2[j] + c1[j]
        to_chip[j].start()

    def close3(j):
        mine = slice(j * RC, (j + 1) * RC)
        to_chip[j].wait_recv()
        hres[mine, :] = (h2[mine, :].astype(F32) + gate0[mine] * (c2[j] + c3[j])).astype(BF)
        own = norm32(hres[mine, :].astype(F32), gain(g4_ref))
        s0[mine, :] = own.astype(F32)
        share[j].start()
        xbuf[j // 2, pl.ds((j % 2) * RC, RC), :] = own

    def shared3(j):
        share[j].wait_recv()
        xbuf[j // 2, pl.ds(HQ + (j % 2) * RC, RC), :] = s1[pl.ds(j * RC, RC), :].astype(BF)

    def cross_out(j):
        lhs = heads_to_lanes(att, (core * NQ + j * RC, (1 - core) * NQ + j * RC), RC)
        for n in range(NCH):
            part = dot(lhs, wo2[:, cols(n)])
            c0[j, :, cols(n)] = part[RC:]
            c2[j, :, cols(n)] = part[:RC]
        to_core[j].start()

    to_y = [[rcopy(fin.at[h, j], yr.at[h, j], gsem.at[h, 0, j], gsem.at[h, 1, j], pe["y"]) for j in range(NCH)]
            for h in range(2)]
    to_c = [[rcopy(fin.at[h, j], cr.at[0, h, j], gsem.at[h, 2, j], gsem.at[h, 3, j], pe["c"]) for j in range(NCH)]
            for h in range(2)]
    pass_c = [[rcopy(yr.at[h, j], cr.at[1, h, j], gsem.at[h, 4, j], gsem.at[h, 5, j], pe["c"]) for j in range(NCH)]
              for h in range(2)]

    def rows(of_sp, of_core, h):
        return pl.ds(pl.multiple_of(of_sp * NH + of_core * NQ + h * HQ, HQ), HQ)

    outs = []

    def put(of_sp, of_core, h):
        r = rows(of_sp, of_core, h)
        outs.append(pltpu.make_async_copy(out_ref.at[r], out_hbm.at[r], rsem.at[len(outs)]))
        outs[-1].start()

    def pass_on(h, j):
        to_y[h][j].wait_recv()
        pass_c[h][j].start()

    def close4(h, passing):
        def done(j, total):
            res = (hres[owned[h], cols(j)].astype(F32) + gate1[owned[h]] * total).astype(BF)
            out_ref[rows(sp, core, h), cols(j)] = res
            fin[h, j] = res.astype(F32)
            to_y[h][j].start()
            to_c[h][j].start()
            if passing is not None:
                pass_on(passing, j)

        sum4[h].close(done)
        put(sp, core, h)

    def gathered(h):
        for j in range(NCH):
            to_c[h][j].wait_recv()
            out_ref[rows(sp, 1 - core, h), cols(j)] = cr[0, h, j].astype(BF)
        put(sp, 1 - core, h)
        for j in range(NCH):
            out_ref[rows(1 - sp, core, h), cols(j)] = yr[h, j].astype(BF)
        put(1 - sp, core, h)
        for j in range(NCH):
            pass_c[h][j].wait_recv()
            out_ref[rows(1 - sp, 1 - core, h), cols(j)] = cr[1, h, j].astype(BF)
        put(1 - sp, 1 - core, h)
        for j in range(NCH):
            to_y[h][j].wait_send()
            to_c[h][j].wait_send()
            pass_c[h][j].wait_send()

    blocks_to = lambda lo, hi: lax.fori_loop(lo, hi, block, 0)
    with jax.named_scope("x0"):
        blocks_to(0, 4)
    with jax.named_scope("o0"):
        cross_out(0)
    with jax.named_scope("x4"):
        blocks_to(4, 5)
    with jax.named_scope("pass0"):
        pass_chip(0)
    with jax.named_scope("x5"):
        blocks_to(5, 7)
    with jax.named_scope("close2_b"):
        close2(1)
    with jax.named_scope("x7"):
        blocks_to(7, 8)
    with jax.named_scope("o1"):
        cross_out(1)
    with jax.named_scope("q_b"):
        cross_q(1)
    with jax.named_scope("x8"):
        blocks_to(8, 9)
    with jax.named_scope("pass1"):
        pass_chip(1)
    with jax.named_scope("close3_0"):
        close3(0)
    with jax.named_scope("x9"):
        blocks_to(9, 12)
    with jax.named_scope("o2"):
        cross_out(2)
    with jax.named_scope("x12"):
        blocks_to(12, 13)
    with jax.named_scope("pass2"):
        pass_chip(2)
    with jax.named_scope("close3_1"):
        close3(1)
    with jax.named_scope("x13"):
        blocks_to(13, 16)
    with jax.named_scope("o3"):
        cross_out(3)
    with jax.named_scope("shared01"):
        shared3(0)
        shared3(1)
        for cp in loads2:
            cp.wait()
    with jax.named_scope("mlp2_a"):
        mlp_act(xbuf.at[0], wg, wu, act.at[0], (0,))
        pass_chip(3)
        mlp_act(xbuf.at[0], wg, wu, act.at[0], (1,))
        close3(2)
        mlp_act(xbuf.at[0], wg, wu, act.at[0], (2,))
        mlp_down(0, sum4[0])
    with jax.named_scope("forward4_a"):
        sum4[0].forward()
    with jax.named_scope("close3_3"):
        close3(3)
    with jax.named_scope("shared23"):
        shared3(2)
        shared3(3)
    with jax.named_scope("mlp2_b"):
        mlp(1, sum4[1])
    with jax.named_scope("forward4_b"):
        sum4[1].forward()
    with jax.named_scope("close4_a"):
        close4(0, None)
    with jax.named_scope("close4_b"):
        close4(1, 0)
    with jax.named_scope("gathered_a"):
        gathered(0)
    with jax.named_scope("gathered_b"):
        for j in range(NCH):
            pass_on(1, j)
        gathered(1)
    for j in range(NCH):
        to_core[j].wait_send()
        to_chip[j].wait_send()
        share[j].wait_send()
    for cp in outs:
        cp.wait()


def rest_of_step(o, st, hidden, g2, g3, qn, g4, gates, mask, xvalid, ws, k_cross, v_cross):
    wo, wg, wu, wd, wq, wo2 = ws[:6]
    F = wg.shape[1]
    T2 = k_cross.shape[1]
    dma = pltpu.SemaphoreType.DMA
    sum_bufs = [pltpu.VMEM((2, NCH, HQ, W), F32)] * 4 + [dma((2, 4, NCH))]
    share_bufs = [pltpu.VMEM((NQ, HID), F32)] * 2 + [dma((2, 2))]
    return pl.pallas_call(
        rest_kernel,
        in_specs=[ANY, VM, ANY, VM, VM, VM, VM, pl.BlockSpec(memory_space=pltpu.SMEM), VM] + [ANY] * 12,
        out_specs=ANY,
        out_shape=jax.ShapeDtypeStruct((NB, HID), BF),
        scratch_shapes=[pltpu.VMEM((NB, HID), BF), dma((8,))] + [pltpu.VMEM(w.shape, BF) for w in (wo, wg, wu, wd, wq, wo2)] + [
            dma((10,)), pltpu.VMEM((NR, CR, T2, D), BF), pltpu.VMEM((NR, CR, T2, D), BF), dma((2, NR)),
            pltpu.VMEM((NH * HL, D), F32), pltpu.VMEM((NH * HL, D), F32), pltpu.VMEM((8, D), F32),
            pltpu.VMEM((8, D), F32), dma((2, 5)), pltpu.VMEM((NQ, HID), BF), pltpu.VMEM((NH * HL, D), F32),
            pltpu.VMEM((NH, xvalid.shape[1]), jnp.int32), pltpu.VMEM((NH, D), jnp.int32),
            pltpu.VMEM((NH * 8, D), F32), pltpu.VMEM((2, NQ, HID), BF), pltpu.VMEM((2, NQ, F), BF),
            pltpu.VMEM((NQ, HID), BF), pltpu.VMEM((NQ, HID), BF), pltpu.VMEM((2, NCH, HQ, W), F32),
            pltpu.VMEM((2, NCH, HQ, W), F32), pltpu.VMEM((2, 2, NCH, HQ, W), F32), dma((2, 6, NCH))]
        + sum_bufs + sum_bufs + [pltpu.VMEM((NCH, RC, HID), F32)] * 4 + [dma((4, NCH)), dma((2, NCH))]
        + share_bufs + share_bufs + [dma((2, 4, NCH))],
        compiler_params=pltpu.CompilerParams(collective_id=0, has_side_effects=True, vmem_limit_bytes=VMEM_MAX),
        name="rest_of_step",
    )(o, st, hidden, g2, g3, qn, g4, gates, mask, xvalid, *ws, k_cross, v_cross)


def solution(mesh):
    cache_spec = P('dp', 'sp', 'tp', None)
    cross_spec = P('dp', None, 'tp', None)
    row_spec = P('dp', None)
    vec_spec = P('dp')
    full_spec = P(None)
    col_spec = P(None, 'tp')
    split_rows = P('tp', None)
    in_specs = (row_spec, vec_spec, cache_spec, cache_spec, cross_spec, cross_spec, row_spec, vec_spec,
                full_spec, col_spec, col_spec, col_spec, split_rows, full_spec, col_spec, col_spec, split_rows,
                full_spec, col_spec, full_spec, split_rows, full_spec, full_spec, col_spec, col_spec, split_rows)
    out_specs = (row_spec, cache_spec, cache_spec)

    def local_step(hidden, new_pos, k_self, v_self, k_cross, v_cross, xvalid, rowmask,
                   self_attn_norm, self_wq, self_wk, self_wv, self_wo, self_mlp_norm,
                   self_wgate, self_wup, self_wdown, cross_attn_norm, cross_wq, cross_qnorm,
                   cross_wo, cross_gates, cross_mlp_norm, cross_wgate, cross_wup, cross_wdown):
        flat = lambda a: a.reshape(a.shape[0], a.shape[1] * a.shape[2], a.shape[3])
        k_out, v_out, o, st = self_attention(new_pos, self_attn_norm, hidden, self_wq, self_wk, self_wv,
                                             flat(k_self), flat(v_self))
        weights = (self_wo, self_wgate, self_wup, self_wdown, cross_wq, cross_wo, cross_wgate, cross_wup, cross_wdown)
        h4 = rest_of_step(o, st, hidden, self_mlp_norm, cross_attn_norm, cross_qnorm, cross_mlp_norm, cross_gates,
                          rowmask, xvalid, weights, flat(k_cross), flat(v_cross))
        return h4, k_out.reshape(k_self.shape), v_out.reshape(v_self.shape)

    return jax.shard_map(local_step, mesh=mesh, in_specs=in_specs, out_specs=out_specs, check_vma=False)
```

profile of v0, /device:TPU:0, one launch (start us, length us, event | category | flops | bytes accessed | tf_op | source)
XLA Modules:
  0.0 108.9 jit_solution(3371985186741498769)
XLA Ops:
  0.6 24.8 %self_attn.1 = (bf16[256,256,128]{2,1,0:T(8,128)(2,1)}, bf16[256,256,128]{2,1,0:T(8,128)(2,1)}, f32[1024,128]{1,0:T(8,128)}, f32[16,128]{1,0:T(8,128)}) custom-call(s32[256]{0:T(256)} %posv_ref.1, s32[256]{0:T(256)} %posv_ref.1, f32[1,128]{1,0:T(1,128)} %constant.2.clone.freq_ref, bf16[2048]{0:T(1024)(128)(2,1)} %g_ref.1, bf16[256,2048]{1,0:T(8,128)(2,1)} %hid_hbm.3, ...), custom_call_target="tpu_custom_call" | custom-call | tf_op jit(solution)/shard_map/self_attn/pallas_call | solution.py:200
  25.4 81.1 %rest_of_step.1 = bf16[256,2048]{1,0:T(8,128)(2,1)} custom-call(f32[1024,128]{1,0:T(8,128)} %get-tuple-element.7.o_hbm, f32[16,128]{1,0:T(8,128)} %get-tuple-element.8.st_ref, bf16[256,2048]{1,0:T(8,128)(2,1)} %hid_hbm.3, bf16[2048]{0:T(1024)(128)(2,1)} %g2_ref.1, bf16[2048]{0:T(1024)(128)(2,1)} %g3_ref.1, bf16[128]{0:T(256)(128)(2,1)} %qn_ref.1, ...), custom_call_target="tpu_custom_call" | custom-call | tf_op jit(solution)/shard_map/rest_of_step/pallas_call | solution.py:648
  106.6 2.3 %copy.31 = bf16[256,2048]{1,0:T(8,128)(2,1)} copy(bf16[256,2048]{1,0:T(8,128)(2,1)} %rest_of_step.1) | data formatting | bytes 2097152
where the time goes:
time: 109 us
  Pallas kernels  106 us (97%)
  local copies, waits for them, and re-layouts  2.3 us (2%)
    pallas_call x1, Pallas kernels, rest_of_step(): pl.pallas_call(rest_kernel, in_specs=[ANY, VM, ANY, VM, VM, VM, VM, pl.Bl...  81.1 us
    pallas_call x1, Pallas kernels, self_attention(): pl.pallas_call(self_kernel, in_specs=[pl.BlockSpec(memory_space=pltpu.SME...  24.8 us
    unnamed x1, local copies, waits for them, and re-layouts  2.3 us

commit v1 on v0

--- a/solution.py
+++ b/solution.py
@@ -430,20 +430,22 @@
         cp.wait()
     with jax.named_scope("mlp_a"):
         mlp(0, sum2[0])
-        sum2[0].forward()
     with jax.named_scope("close1_b"):
         close1(1)
+    with jax.named_scope("forward2_a"):
+        sum2[0].forward()
     with jax.named_scope("share1_b"):
         share1[1].finish()
     with jax.named_scope("mlp_b"):
         mlp(1, sum2[1])
-        sum2[1].forward()
     loads2 = [pltpu.make_async_copy(a, b, wsem.at[1 + n])
               for n, (a, b) in enumerate(((wg2_hbm, wg), (wu2_hbm, wu), (wd2_hbm, wd)))]
     for cp in loads2:
         cp.start()
     with jax.named_scope("close2_a"):
         close2(0)
+    with jax.named_scope("forward2_b"):
+        sum2[1].forward()
     loads[4].wait()
     with jax.named_scope("q_a"):
         cross_q(0)

time: 109 us -> 109 us (level)
  no operation moved by 1% of the time
where the time goes in v1:
time: 109 us
  Pallas kernels  106 us (97%)
  local copies, waits for them, and re-layouts  2.3 us (2%)
    pallas_call x1, Pallas kernels, rest_of_step(): pl.pallas_call(rest_kernel, in_specs=[ANY, VM, ANY, VM, VM, VM, VM, pl.Bl...  81 us
    pallas_call x1, Pallas kernels, self_attention(): pl.pallas_call(self_kernel, in_specs=[pl.BlockSpec(memory_space=pltpu.SME...  24.8 us
    unnamed x1, local copies, waits for them, and re-layouts  2.3 us

profile of v1, /device:TPU:0, one launch (start us, length us, event | category | flops | bytes accessed | tf_op | source)
XLA Modules:
  0.0 108.8 jit_solution(2309805519476270123)
XLA Ops:
  0.6 24.8 %self_attn.1 = (bf16[256,256,128]{2,1,0:T(8,128)(2,1)}, bf16[256,256,128]{2,1,0:T(8,128)(2,1)}, f32[1024,128]{1,0:T(8,128)}, f32[16,128]{1,0:T(8,128)}) custom-call(s32[256]{0:T(256)} %posv_ref.1, s32[256]{0:T(256)} %posv_ref.1, f32[1,128]{1,0:T(1,128)} %constant.2.clone.freq_ref, bf16[2048]{0:T(1024)(128)(2,1)} %g_ref.1, bf16[256,2048]{1,0:T(8,128)(2,1)} %hid_hbm.3, ...), custom_call_target="tpu_custom_call" | custom-call | tf_op jit(solution)/shard_map/self_attn/pallas_call | solution.py:200
  25.4 81.0 %rest_of_step.1 = bf16[256,2048]{1,0:T(8,128)(2,1)} custom-call(f32[1024,128]{1,0:T(8,128)} %get-tuple-element.7.o_hbm, f32[16,128]{1,0:T(8,128)} %get-tuple-element.8.st_ref, bf16[256,2048]{1,0:T(8,128)(2,1)} %hid_hbm.3, bf16[2048]{0:T(1024)(128)(2,1)} %g2_ref.1, bf16[2048]{0:T(1024)(128)(2,1)} %g3_ref.1, bf16[128]{0:T(256)(128)(2,1)} %qn_ref.1, ...), custom_call_target="tpu_custom_call" | custom-call | tf_op jit(solution)/shard_map/rest_of_step/pallas_call | solution.py:650
  106.5 2.3 %copy.31 = bf16[256,2048]{1,0:T(8,128)(2,1)} copy(bf16[256,2048]{1,0:T(8,128)(2,1)} %rest_of_step.1) | data formatting | bytes 2097152
